TPU v7x, 32 devices: a whole 2x2x4 slice. The times are simulated.
32 devices in a mesh: groups: 2 (over y), seq: 16 (over z, x, core).
Axes of the slice: x: 2, y: 2, z: 4, core: 2. Of those that a mesh axis runs over, the one named last changes fastest.
Arguments:
- queries: bfloat16 [8192, 2048], P(('groups', 'seq')), parts along dimension 0, may hold values from -20 to 20
- keys: bfloat16 [8192, 2048], P(('groups', 'seq')), parts along dimension 0, may hold values from -20 to 20
- values: bfloat16 [8192, 2048], P(('groups', 'seq')), parts along dimension 0, may hold values from -6 to 6
- block_counts: int32 [16], P('groups'), parts along dimension 0, may hold values from 2 to 6, as said below
- last_tokens: int32 [32], P('groups'), parts along dimension 0, may hold values from 64 to 128
- pack_order: int32 [32], P('groups'), parts along dimension 0, may hold values from 0 to 15, as said below
- decode_slot: int32 [16], P('groups'), parts along dimension 0, may hold values from 0 to 7, each once
Outputs:
- attended: bfloat16 [8192, 2048], P(('groups', 'seq')), parts along dimension 0
- cache_keys: bfloat16 [32, 32, 128, 128], P(('groups', 'seq')), parts along dimension 0
- cache_values: bfloat16 [32, 32, 128, 128], P(('groups', 'seq')), parts along dimension 0
There are 2 independent parts, one for each index of `groups`. A program takes and returns all parts, laid end to end along the dimension named above; each array names one. Nothing has to cross between parts.
Inputs may be any that keep to these rules, and one draw needn't show every extreme that they name: `block_counts`: they sum to 24; the largest equals 6. `pack_order`: each prompt number appears once. The last 1 positions hold null prompts, and the position before them a conditional prompt of 6 blocks. `decode_slot`: each slot appears once.
All inputs are finite; a program needn't handle non-finite values.
Results may differ from a plain program's by a relative error of at most 0.0034.
Values may be sent and summed in bfloat16 or wider, within the bound.
A program may use at most 64 MiB of HBM per device.

v0:
```python
import jax
import jax.numpy as jnp
from jax import lax
from jax.sharding import PartitionSpec as P

HEADS = 16
HEAD_DIM = 128
BLOCK = 128
MAXB = 6


MASKED_SCORE = -1e30


def shifted(block, axis, distance):
    devices = range(lax.axis_size(axis))
    route = [(i - distance, i) for i in devices if i - distance in devices]
    return lax.ppermute(block, axis, route)


def block_tables(block_counts, last_tokens, pack_order, decode_slot, total_blocks, block):
    pair_count = block_counts.shape[0]
    prompts = 2 * pair_count
    prompt_ids = jnp.arange(prompts, dtype=jnp.int32)
    prompt_sizes = jnp.concatenate([block_counts, jnp.ones((pair_count,), jnp.int32)])
    picked = (pack_order[:, None] == prompt_ids[None, :]).astype(jnp.int32)
    packed_sizes = jnp.sum(picked * prompt_sizes[None, :], axis=1)
    packed_tails = jnp.sum(picked * last_tokens[None, :], axis=1)
    block_ends = jnp.cumsum(packed_sizes)
    starts = block_ends - packed_sizes
    blocks = jnp.arange(total_blocks, dtype=jnp.int32)
    member = (
        (starts[None, :] <= blocks[:, None]) & (blocks[:, None] < block_ends[None, :])
    ).astype(jnp.int32)
    position = jnp.sum(member * prompt_ids[None, :], axis=1)
    prompt = jnp.sum(member * pack_order[None, :], axis=1)
    within = blocks - jnp.sum(member * starts[None, :], axis=1)
    is_last = blocks + 1 == jnp.sum(member * block_ends[None, :], axis=1)
    valid_tokens = jnp.where(is_last, jnp.sum(member * packed_tails[None, :], axis=1), block)
    pair_ids = jnp.arange(pair_count, dtype=jnp.int32)
    earlier = (decode_slot[None, :] < decode_slot[:, None]).astype(jnp.int32)
    slot_start = jnp.sum(earlier * (block_counts + 1)[None, :], axis=1)
    pair_of = prompt % pair_count
    owner = (pair_of[:, None] == pair_ids[None, :]).astype(jnp.int32)
    base_slot = jnp.sum(owner * slot_start[None, :], axis=1)
    own_count = jnp.sum(owner * block_counts[None, :], axis=1)
    destination = base_slot + jnp.where(prompt >= pair_count, own_count, within)
    hits = (destination[None, :] == blocks[:, None]).astype(jnp.int32)
    source = jnp.sum(hits * blocks[None, :], axis=1)
    return (position, valid_tokens, source)


def hand_off(paired, source, devices):
    tokens_here = paired.shape[1]
    blocks_here = tokens_here // BLOCK
    splits = devices // HEADS
    slice_len = BLOCK // splits
    outgoing = paired.reshape(2, blocks_here, splits, slice_len, HEADS, HEAD_DIM)
    outgoing = jnp.transpose(outgoing, (4, 2, 0, 1, 3, 5)).reshape(
        devices, 2, blocks_here, slice_len, HEAD_DIM
    )
    arrived = lax.all_to_all(outgoing, "seq", split_axis=0, concat_axis=2, tiled=True)
    ordered = jnp.take(arrived[0], source, axis=1)
    return (ordered[0][None], ordered[1][None])


def attend(queries, paired, position, valid_tokens, own_index, reach):
    tokens_here, features = queries.shape
    blocks_here = tokens_here // BLOCK
    pieces = [paired]
    current = paired
    for distance in range(reach):
        current = shifted(current, "seq", 1)
        pieces.insert(0, current)
    prior_count = reach * blocks_here
    window = jnp.concatenate(pieces, axis=1)
    window_blocks = prior_count + blocks_here
    lead_blocks = reach * blocks_here
    padded_docs = jnp.concatenate([jnp.full((lead_blocks,), -1, jnp.int32), position])
    padded_valid = jnp.concatenate([jnp.zeros((lead_blocks,), jnp.int32), valid_tokens])
    first_block = own_index * blocks_here + lead_blocks - prior_count
    window_docs = lax.dynamic_slice_in_dim(padded_docs, first_block, window_blocks)
    window_valid = lax.dynamic_slice_in_dim(padded_valid, first_block, window_blocks)
    own_first = own_index * blocks_here
    query_docs = lax.dynamic_slice_in_dim(position, own_first, blocks_here)
    query_valid = lax.dynamic_slice_in_dim(valid_tokens, own_first, blocks_here)
    token_ids = jnp.arange(BLOCK, dtype=jnp.int32)
    key_docs = jnp.repeat(window_docs, BLOCK)
    key_limit = jnp.repeat(window_valid, BLOCK)
    key_tokens = jnp.tile(token_ids, window_blocks)
    key_order = jnp.arange(window_blocks * BLOCK, dtype=jnp.int32) - prior_count * BLOCK
    query_order = jnp.arange(tokens_here, dtype=jnp.int32)
    allowed = key_docs[None, :] == jnp.repeat(query_docs, BLOCK)[:, None]
    allowed = (
        allowed & (key_order[None, :] <= query_order[:, None]) & (key_tokens < key_limit)[None, :]
    )
    query_ok = jnp.tile(token_ids, blocks_here) < jnp.repeat(query_valid, BLOCK)
    score_scale = HEAD_DIM ** (-0.5)
    query_heads = jnp.moveaxis(queries.reshape(tokens_here, HEADS, HEAD_DIM), 1, 0)
    key_heads = jnp.moveaxis(window[0].reshape(-1, HEADS, HEAD_DIM), 1, 0)
    value_heads = jnp.moveaxis(window[1].reshape(-1, HEADS, HEAD_DIM), 1, 0)

    def one_head(operands):
        query_part, key_part, value_part = operands
        scores = (
            jnp.einsum("qd,kd->qk", query_part, key_part, preferred_element_type=jnp.float32)
            * score_scale
        )
        scores = jnp.where(allowed, scores, MASKED_SCORE)
        peak = jnp.max(scores, axis=1, keepdims=True)
        weights = jnp.exp(scores - peak)
        totals = jnp.sum(weights, axis=1, keepdims=True)
        mixed = jnp.dot(
            weights.astype(jnp.bfloat16), value_part, preferred_element_type=jnp.float32
        )
        return mixed / totals

    head_outputs = lax.map(one_head, (query_heads, key_heads, value_heads))
    merged = jnp.moveaxis(head_outputs, 0, 1).reshape(tokens_here, features)
    return jnp.where(query_ok[:, None], merged, 0.0).astype(jnp.bfloat16)


def local(queries, keys, values, block_counts, last_tokens, pack_order, decode_slot):
    devices = lax.axis_size("seq")
    own_index = lax.axis_index("seq")
    tokens_here = queries.shape[0]
    blocks_here = tokens_here // BLOCK
    reach = (MAXB + blocks_here - 2) // blocks_here
    position, valid_tokens, source = block_tables(
        block_counts, last_tokens, pack_order, decode_slot, blocks_here * devices, BLOCK
    )
    paired = jnp.stack([keys, values])
    attended = attend(queries, paired, position, valid_tokens, own_index, reach)
    cache_keys, cache_values = hand_off(paired, source, devices)
    return (attended, cache_keys, cache_values)


def solution(mesh):
    placed = (
        P(("groups", "seq"), None),
        P(("groups", "seq"), None),
        P(("groups", "seq"), None),
        P("groups"),
        P("groups"),
        P("groups"),
        P("groups"),
    )
    return jax.shard_map(
        local,
        mesh=mesh,
        in_specs=placed,
        out_specs=(
            P(("groups", "seq"), None),
            P(("groups", "seq"), None, None, None),
            P(("groups", "seq"), None, None, None),
        ),
        check_vma=False,
    )
```

profile of v0, /device:TPU:20, one launch (start us, length us, event | category | flops | bytes accessed | tf_op | source)
XLA Modules:
  0.0 189.0 jit_solution(15952049757768567406)
XLA Ops:
  0.6 1.6 copy.47
  4.2 1.9 %collective-permute-start = (bf16[2,256,2048]{1,2,0:T(8,128)(2,1)}, bf16[2,256,2048]{1,2,0:T(8,128)(2,1)}, u32[]{:S(2)}, u32[]{:S(2)}) collective-permute-start(bf16[2,256,2048]{1,2,0:T(8,128)(2,1)} %pad_maximum_fusion), channel_id=1, source_target_pairs={{0,1},{1,2},{2,3},{3,4},{4,5},{5,6},{6,7},{7,8},{8,9},{9,10},{10,1... | collective-permute-start | bytes 6291464 | tf_op jit(solution)/shard_map/ppermute | solution.py:18
  6.8 1.9 %copy.53 = bf16[16,2,2,128,128]{4,3,2,1,0:T(8,128)(2,1)} copy(bf16[16,2,2,128,128]{4,0,3,2,1:T(8,128)(2,1)S(1)} %maximum_bitcast_fusion) | data formatting | bytes 4194304 | tf_op jit(solution)/shard_map/reshape | solution.py:59
  8.8 6.6 %all-to-all-start = ((bf16[16,2,2,128,128]{4,3,2,1,0:T(8,128)(2,1)}), bf16[16,2,2,128,128]{4,3,2,1,0:T(8,128)(2,1)}, u32[]{:S(2)}, u32[]{:S(2)}) async-start(bf16[16,2,2,128,128]{4,3,2,1,0:T(8,128)(2,1)} %copy.53), calls=%async_computation | async-start | bytes 4194304 | tf_op jit(solution)/shard_map/all_to_all | solution.py:62
  15.4 51.1 %collective-permute-done = bf16[2,256,2048]{1,2,0:T(8,128)(2,1)} collective-permute-done((bf16[2,256,2048]{1,2,0:T(8,128)(2,1)}, bf16[2,256,2048]{1,2,0:T(8,128)(2,1)}, u32[]{:S(2)}, u32[]{:S(2)}) %collective-permute-start) | collective-permute-done | bytes 2097184 | tf_op jit(solution)/shard_map/ppermute | solution.py:18
  66.5 1.9 %collective-permute-start.1 = (bf16[2,256,2048]{1,2,0:T(8,128)(2,1)}, bf16[2,256,2048]{1,2,0:T(8,128)(2,1)}, u32[]{:S(2)}, u32[]{:S(2)}) collective-permute-start(bf16[2,256,2048]{1,2,0:T(8,128)(2,1)} %collective-permute-done), channel_id=1, source_target_pairs={{0,1},{1,2},{2,3},{3,4},{4,5},{5,6},{6,7},{7,8},{8,9},{9,10},{10,1... | collective-permute-start | bytes 6291464 | tf_op jit(solution)/shard_map/ppermute | solution.py:18
  69.5 30.8 %collective-permute-done.1 = bf16[2,256,2048]{1,2,0:T(8,128)(2,1)} collective-permute-done((bf16[2,256,2048]{1,2,0:T(8,128)(2,1)}, bf16[2,256,2048]{1,2,0:T(8,128)(2,1)}, u32[]{:S(2)}, u32[]{:S(2)}) %collective-permute-start.1) | collective-permute-done | bytes 2097184 | tf_op jit(solution)/shard_map/ppermute | solution.py:18
  100.3 1.9 %collective-permute-start.2 = (bf16[2,256,2048]{1,2,0:T(8,128)(2,1)}, bf16[2,256,2048]{1,2,0:T(8,128)(2,1)}, u32[]{:S(2)}, u32[]{:S(2)}) collective-permute-start(bf16[2,256,2048]{1,2,0:T(8,128)(2,1)} %collective-permute-done.1), channel_id=1, source_target_pairs={{0,1},{1,2},{2,3},{3,4},{4,5},{5,6},{6,7},{7,8},{8,9},{9,10},{10,1... | collective-permute-start | bytes 6291464 | tf_op jit(solution)/shard_map/ppermute | solution.py:18
  102.5 2.3 %copy.46 = bf16[256,2048]{0,1:T(8,128)(2,1)} copy(bf16[256,2048]{1,0:T(8,128)(2,1)} %param.9) | data formatting | bytes 2097152 | tf_op args[0]
  105.0 3.2 %copy.54 = bf16[16,2,2,128,128]{4,3,2,0,1:T(8,128)(2,1)} copy(bf16[16,2,2,128,128]{4,3,2,1,0:T(8,128)(2,1)} %all-to-all-done) | data formatting | bytes 4194304 | tf_op jit(solution)/shard_map/all_to_all | solution.py:62
  108.3 3.7 %gather_fusion = bf16[32,2,128,128]{3,2,1,0:T(8,128)(2,1)} fusion(bf16[2,32,128,128]{3,2,1,0:T(8,128)(2,1)} %bitcast.87, s32[1024]{0:T(1024)S(1)} %pad_clamp_fusion), kind=kCustom, calls=%fused_computation | custom fusion | bytes 4194432 | tf_op jit(solution)/shard_map/jit(_take)/gather | solution.py:63
  112.0 1.8 select_bitcast_fusion
  115.3 13.6 %collective-permute-done.2 = bf16[2,256,2048]{1,2,0:T(8,128)(2,1)} collective-permute-done((bf16[2,256,2048]{1,2,0:T(8,128)(2,1)}, bf16[2,256,2048]{1,2,0:T(8,128)(2,1)}, u32[]{:S(2)}, u32[]{:S(2)}) %collective-permute-start.2) | collective-permute-done | bytes 2097184 | tf_op jit(solution)/shard_map/ppermute | solution.py:18
  128.9 3.9 %maximum_maximum_fusion = bf16[2,1024,2048]{1,2,0:T(8,128)(2,1)S(1)} fusion(bf16[1,256,2048]{1,2,0:T(8,128)(2,1)S(1)} %bitcast.86, bf16[1,256,2048]{1,2,0:T(8,128)(2,1)S(1)} %bitcast.84, bf16[2,256,2048]{1,2,0:T(8,128)(2,1)} %collective-permute-done, bf16[2,256,2048]{1,2,0:T(8,128)(2,1)} %collective-permute-done.1, ...), kind=kLoop, calls=%fused_computation.22 | loop fusion | flops 41943040 | bytes 16777216 | tf_op jit(solution)/shard_map/concatenate | solution.py:76
  132.8 3.7 %fusion.26 = (bf16[1,1024,2048]{1,2,0:T(8,128)(2,1)}, bf16[1,1024,2048]{1,2,0:T(8,128)(2,1)}) fusion(bf16[2,1024,2048]{1,2,0:T(8,128)(2,1)S(1)} %maximum_maximum_fusion), kind=kLoop, calls=%fused_computation.69 | loop fusion | bytes 16777216 | tf_op jit(solution)/shard_map/slice | solution.py:101
  136.4 51.3 %while.11 = (s32[]{:T(128)}, bf16[16,256,128]{2,1,0:T(8,128)(2,1)S(1)}, bf16[16,256,128]{1,2,0:T(8,128)(2,1)}, bf16[16,1024,128]{1,2,0:T(8,128)(2,1)}, bf16[16,1...) while((s32[]{:T(128)}, ...), condition=%wide.region_9.10_spmd.clone, body=%wide.region_6.0_spmd.clone.sunk | while | flops 137133568 | bytes 3884133 | solution.py:118
  136.4 1.5 fusion.35
  139.6 1.5 fusion.35
  142.9 1.5 fusion.35
  146.1 1.5 fusion.35
  149.3 1.5 fusion.35
  152.5 1.5 fusion.35
  155.7 1.5 fusion.35
  158.9 1.5 fusion.35
  162.1 1.5 fusion.35
  165.3 1.5 fusion.35
  168.5 1.5 fusion.35
  171.7 1.5 fusion.35
  174.9 1.5 fusion.35
  178.1 1.5 fusion.35
  181.4 1.5 fusion.35
  184.6 1.5 fusion.35
  (78 shorter events, 33.2 us)
Async XLA Ops:
  0.6 1.6 copy-start.1
  2.8 3.4 %copy-start = (bf16[256,2048]{1,0:T(8,128)(2,1)S(1)}, bf16[256,2048]{1,0:T(8,128)(2,1)}, u32[]{:S(2)}) copy-start(bf16[256,2048]{1,0:T(8,128)(2,1)} %param.10) | copy-start | bytes 3145732
  4.2 62.3 %collective-permute-start = (bf16[2,256,2048]{1,2,0:T(8,128)(2,1)}, bf16[2,256,2048]{1,2,0:T(8,128)(2,1)}, u32[]{:S(2)}, u32[]{:S(2)}) collective-permute-start(bf16[2,256,2048]{1,2,0:T(8,128)(2,1)} %pad_maximum_fusion), channel_id=1, source_target_pairs={{0,1},{1,2},{2,3},{3,4},{4,5},{5,6},{6,7},{7,8},{8,9},{9,10},{10,1... | collective-permute-start | bytes 6291464 | tf_op jit(solution)/shard_map/ppermute | solution.py:18
  8.8 59.6 %copy-start.5 = (s32[8]{0:T(128)S(1)}, s32[8]{0:T(128)}, u32[]{:S(2)}) copy-start(s32[8]{0:T(128)} %param.12) | copy-start | bytes 100
  8.8 59.7 %copy-start.2 = (s32[16]{0:T(128)S(1)}, s32[16]{0:T(128)}, u32[]{:S(2)}) copy-start(s32[16]{0:T(128)} %param.14) | copy-start | bytes 196
  8.8 59.7 %copy-start.4 = (s32[16]{0:T(128)S(1)}, s32[16]{0:T(128)}, u32[]{:S(2)}) copy-start(s32[16]{0:T(128)} %param.13) | copy-start | bytes 196
  8.8 60.3 %copy-start.3 = (s32[8]{0:T(128)S(1)}, s32[8]{0:T(128)}, u32[]{:S(2)}) copy-start(s32[8]{0:T(128)} %param.15) | copy-start | bytes 100
  8.8 96.2 %all-to-all-start = ((bf16[16,2,2,128,128]{4,3,2,1,0:T(8,128)(2,1)}), bf16[16,2,2,128,128]{4,3,2,1,0:T(8,128)(2,1)}, u32[]{:S(2)}, u32[]{:S(2)}) async-start(bf16[16,2,2,128,128]{4,3,2,1,0:T(8,128)(2,1)} %copy.53), calls=%async_computation | async-start | bytes 4194304 | tf_op jit(solution)/shard_map/all_to_all | solution.py:62
  66.5 33.8 %collective-permute-start.1 = (bf16[2,256,2048]{1,2,0:T(8,128)(2,1)}, bf16[2,256,2048]{1,2,0:T(8,128)(2,1)}, u32[]{:S(2)}, u32[]{:S(2)}) collective-permute-start(bf16[2,256,2048]{1,2,0:T(8,128)(2,1)} %collective-permute-done), channel_id=1, source_target_pairs={{0,1},{1,2},{2,3},{3,4},{4,5},{5,6},{6,7},{7,8},{8,9},{9,10},{10,1... | collective-permute-start | bytes 6291464 | tf_op jit(solution)/shard_map/ppermute | solution.py:18
  100.3 28.6 %collective-permute-start.2 = (bf16[2,256,2048]{1,2,0:T(8,128)(2,1)}, bf16[2,256,2048]{1,2,0:T(8,128)(2,1)}, u32[]{:S(2)}, u32[]{:S(2)}) collective-permute-start(bf16[2,256,2048]{1,2,0:T(8,128)(2,1)} %collective-permute-done.1), channel_id=1, source_target_pairs={{0,1},{1,2},{2,3},{3,4},{4,5},{5,6},{6,7},{7,8},{8,9},{9,10},{10,1... | collective-permute-start | bytes 6291464 | tf_op jit(solution)/shard_map/ppermute | solution.py:18
where the time goes:
time: 190 us; the launch traced here: 189 us
  waiting for transfers between devices  95.5 us (50%)
  matrix products  46.1 us (24%)
  local copies, waits for them, and re-layouts  19.4 us (10%)
  other arithmetic  14.5 us (8%)
  starting transfers between devices  12.3 us (6%)
    ppermute x3, waiting for transfers between devices, shifted(): return lax.ppermute(block, axis, route)  95.5 us
    dot_general x16, matrix products, one_head(): jnp.einsum('qd,kd->qk', query_part, key_part, preferred_element_type=jnp....  24.7 us
    dot_general x16, matrix products, one_head(): jnp.dot(weights.astype(jnp.bfloat16), value_part, preferred_element_type=...  21.4 us
    all_to_all x1, starting transfers between devices, hand_off(): lax.all_to_all(outgoing, 'seq', split_axis=0, concat_axis=2, tiled=True)  6.57 us
    unnamed x18, local copies, waits for them, and re-layouts  6.28 us
    ppermute x3, starting transfers between devices, shifted(): return lax.ppermute(block, axis, route)  5.73 us
    reduce_sum x16, other arithmetic, one_head(): totals = jnp.sum(weights, axis=1, keepdims=True)  4.88 us
    concatenate x1, other arithmetic, attend(): window = jnp.concatenate(pieces, axis=1)  3.88 us
  transfers between devices with their start and end apart: 4, of which 3 were waited for; matrix products, arithmetic and copies ran while one was open for 9% of the time, Pallas kernels for 0%

commit v1 on v0

v1 whole, which is shorter than its diff:
```python
import functools
import math

import jax
import jax.numpy as jnp
from jax import lax
from jax.experimental import pallas as pl
from jax.experimental.pallas import tpu as pltpu
from jax.sharding import PartitionSpec as P

HEADS = 16
HEAD_DIM = 128
BLOCK = 128
MAXB = 6
BACK = MAXB - 1
HIDDEN = -1e30
PLANE = 4


def window_tables(counts_ref, tails_ref, order_ref, first, width):
    pairs = counts_ref.shape[0]
    prompts = order_ref.shape[0]

    def place(i, carry):
        start, docs, valids = carry
        prompt = order_ref[i]
        counted = counts_ref[lax.rem(prompt, pairs)]
        size = jnp.where(prompt < pairs, counted, 1)
        tail = tails_ref[prompt]
        end = start + size
        new_docs, new_valids = [], []
        for w in range(width):
            b = first + w
            inside = (start <= b) & (b < end)
            new_docs.append(jnp.where(inside, i, docs[w]))
            new_valids.append(
                jnp.where(inside, jnp.where(b + 1 == end, tail, BLOCK), valids[w])
            )
        return end, tuple(new_docs), tuple(new_valids)

    none = jnp.int32(-1)
    zero = jnp.int32(0)
    _, docs, valids = lax.fori_loop(
        0, prompts, place, (zero, (none,) * width, (zero,) * width)
    )
    return docs, valids


def exchange(
    n,
    counts_ref,
    tails_ref,
    order_ref,
    q_ref,
    k_ref,
    v_ref,
    out_ref,
    landed_ref,
    hk,
    hv,
    relay,
    bias,
    halo_send,
    halo_recv,
    relay_recv,
    cache_send,
    cache_recv,
    own_sem,
):
    me = lax.axis_index("seq")
    role = lax.rem(me, PLANE)
    plane = me // PLANE
    planes = n // PLANE
    tokens = q_ref.shape[0]
    here = tokens // BLOCK
    splits = n // HEADS
    part = BLOCK // splits

    barrier = pltpu.get_barrier_semaphore()

    def greet(r, carry):
        pl.semaphore_signal(
            barrier,
            inc=1,
            device_id={"seq": lax.rem(me + r, n)},
            device_id_type=pl.DeviceIdType.MESH,
        )
        return carry

    lax.fori_loop(1, n, greet, 0)
    pl.semaphore_wait(barrier, n - 1)

    own = (k_ref, v_ref)
    halo = (hk, hv)
    pending = []

    def rows(block):
        return pl.ds(block * BLOCK, BLOCK)

    def send(cond, kv, src, target, slot):
        index = len(pending)
        if slot is None:
            dst, recv = relay.at[kv], relay_recv.at[kv]
        else:
            dst, recv = halo[kv].at[rows(slot)], halo_recv.at[kv, slot]
        copy = pltpu.make_async_remote_copy(
            src_ref=src,
            dst_ref=dst,
            send_sem=halo_send.at[index],
            recv_sem=recv,
            device_id={"seq": lax.rem(target + n, n)},
            device_id_type=pl.DeviceIdType.MESH,
        )
        pending.append((cond, copy))
        return copy

    def start(cond, moves):
        copies = [
            send(cond, kv, src(kv), target, slot)
            for src, target, slot in moves
            for kv in range(2)
        ]

        @pl.when(cond)
        def _():
            for copy in copies:
                copy.start()

    def mine(block):
        return lambda kv: own[kv].at[rows(block)]

    def held(slot):
        return lambda kv: halo[kv].at[rows(slot)]

    def await_slots(cond, slots):
        @pl.when(cond)
        def _():
            for slot in slots:
                for kv in range(2):
                    if slot is None:
                        ref, sem = relay.at[kv], relay_recv.at[kv]
                    else:
                        ref, sem = halo[kv].at[rows(slot)], halo_recv.at[kv, slot]
                    pltpu.make_async_copy(ref, ref, sem).wait()

    more = plane < planes - 1
    late = plane > 0
    start((role == 3) & more, [(mine(1), me + 3, 0), (mine(0), me + 3, None)])
    start((role == 2) & more, [(mine(1), me + 2, 2), (mine(0), me + 2, 1)])
    start((role == 1) & more, [(mine(1), me + 3, 0)])
    start(role == 1, [(mine(0), me + 1, 3), (mine(1), me + 1, 4)])
    start(role == 0, [(mine(1), me + 2, 2), (mine(0), me + 2, 1)])
    start(
        (role == 0) | (role == 2), [(mine(0), me + 1, 3), (mine(1), me + 1, 4)]
    )

    def piece(ref, owner, block):
        head = owner // splits
        cols = pl.ds(pl.multiple_of(head * HEAD_DIM, HEAD_DIM), HEAD_DIM)
        if splits == 1:
            return ref.at[:, cols]
        offset = pl.multiple_of(block * BLOCK + lax.rem(owner, splits) * part, part)
        return ref.at[pl.ds(offset, part), cols]

    def place(kv, block):
        if splits == 1:
            return landed_ref.at[kv, pl.ds(pl.multiple_of(me * tokens, tokens), tokens)]
        return landed_ref.at[
            kv, pl.ds(pl.multiple_of((me * here + block) * part, part), part)
        ]

    pieces = 1 if splits == 1 else here

    def give(s, carry):
        sign = 1 - 2 * lax.rem(s, 2)
        target = lax.rem(me + n // 2 + sign * ((s + 1) // 2), n)
        for kv in range(2):
            for block in range(pieces):
                pltpu.make_async_remote_copy(
                    src_ref=piece(own[kv], target, block),
                    dst_ref=place(kv, block),
                    send_sem=cache_send.at[kv],
                    recv_sem=cache_recv.at[kv],
                    device_id={"seq": target},
                    device_id_type=pl.DeviceIdType.MESH,
                ).start()
        return carry

    far = n - 1 - 2 * (PLANE - 1)
    lax.fori_loop(0, far, give, 0)

    await_slots((role == 2) & late, [0, None])
    start(
        (role == 2) & late,
        [(held(0), me - 2 + n, 4), (lambda kv: relay.at[kv], me - 2 + n, 3)],
    )
    await_slots(role == 2, [2, 3, 4])
    start(role == 2, [(held(2), me + 1, 0), (held(3), me + 1, 1), (held(4), me + 1, 2)])
    await_slots((role == 0) & late, [2, 3, 4])
    start(
        (role == 0) & late,
        [(held(2), me + 1, 0), (held(3), me + 1, 1), (held(4), me + 1, 2)],
    )
    lax.fori_loop(far, n - 1, give, 0)
    local = [
        pltpu.make_async_copy(
            piece(own[kv], me, block), place(kv, block), own_sem.at[kv, block]
        )
        for kv in range(2)
        for block in range(pieces)
    ]
    for copy in local:
        copy.start()

    docs, valids = window_tables(
        counts_ref, tails_ref, order_ref, me * here - BACK, BACK + here
    )
    row = lax.broadcasted_iota(jnp.int32, (BLOCK, BLOCK), 0)
    col = lax.broadcasted_iota(jnp.int32, (BLOCK, BLOCK), 1)
    for b in range(here):
        for w in range(BACK + here):
            if w > BACK + b:
                shade = jnp.full((BLOCK, BLOCK), HIDDEN, jnp.float32)
            else:
                limit = jnp.where(docs[w] == docs[BACK + b], valids[w], 0)
                seen = col < limit
                if w == BACK + b:
                    seen = seen & (col <= row)
                shade = jnp.where(seen, 0.0, HIDDEN)
            bias[b * BLOCK : (b + 1) * BLOCK, w * BLOCK : (w + 1) * BLOCK] = shade
    column = lax.broadcasted_iota(jnp.int32, (BLOCK, HEAD_DIM), 0)
    real = jnp.concatenate(
        [column < valids[BACK + b] for b in range(here)], axis=0
    )

    empty = jnp.zeros((BLOCK, hk.shape[1]), hk.dtype)
    for slot, reach in ((0, 3), (1, 2), (2, 2), (3, 1), (4, 1)):

        @pl.when(me < reach)
        def _():
            for kv in range(2):
                halo[kv][slot * BLOCK : (slot + 1) * BLOCK, :] = empty

    await_slots((role == 0) & late, [0, 1])
    await_slots(role == 1, [3, 4])
    await_slots((role == 1) & late, [0, 1, 2])
    await_slots(role == 2, [1])
    await_slots(role == 3, [0, 1, 2, 3, 4])

    factor = HEAD_DIM ** (-0.5) * math.log2(math.e)
    prior = BACK * BLOCK
    nt = (((1,), (1,)), ((), ()))

    def one_head(h, carry):
        cols = pl.ds(pl.multiple_of(h * HEAD_DIM, HEAD_DIM), HEAD_DIM)
        q = q_ref[:, cols]
        s1 = lax.dot_general(q, hk[:, cols], nt, preferred_element_type=jnp.float32)
        s2 = lax.dot_general(q, k_ref[:, cols], nt, preferred_element_type=jnp.float32)
        s1 = s1 + bias[:, :prior]
        s2 = s2 + bias[:, prior:]
        peak = jnp.maximum(
            jnp.max(s1, axis=1, keepdims=True), jnp.max(s2, axis=1, keepdims=True)
        )
        w1 = jnp.exp2((s1 - peak) * factor)
        w2 = jnp.exp2((s2 - peak) * factor)
        total = jnp.sum(w1, axis=1, keepdims=True) + jnp.sum(w2, axis=1, keepdims=True)
        mixed = jnp.dot(
            w1.astype(jnp.bfloat16), hv[:, cols], preferred_element_type=jnp.float32
        ) + jnp.dot(
            w2.astype(jnp.bfloat16), v_ref[:, cols], preferred_element_type=jnp.float32
        )
        out_ref[:, cols] = jnp.where(real, mixed / total, 0.0).astype(out_ref.dtype)
        return carry

    lax.fori_loop(0, HEADS, one_head, 0)

    for cond, copy in pending:

        @pl.when(cond)
        def _():
            copy.wait_send()

    for copy in local:
        copy.wait()
    others = landed_ref.shape[1] // n * (n - 1)
    for kv in range(2):
        ref = landed_ref.at[kv, pl.ds(0, others)]
        pltpu.make_async_copy(ref, ref, cache_send.at[kv]).wait()
        pltpu.make_async_copy(ref, ref, cache_recv.at[kv]).wait()


def reorder(
    counts_ref,
    order_ref,
    slot_ref,
    landed_ref,
    keys_ref,
    values_ref,
    staged,
    who,
    base,
    in_sem,
    out_sem,
):
    pairs = counts_ref.shape[0]
    prompts = order_ref.shape[0]
    blocks, part = staged.shape[1:3]

    def invert(p, carry):
        who[slot_ref[p]] = p
        return carry

    lax.fori_loop(0, pairs, invert, 0)

    def lay(s, first):
        p = who[s]
        base[p] = first
        return first + counts_ref[p] + 1

    lax.fori_loop(0, pairs, lay, jnp.int32(0))

    def fetch(i, first):
        prompt = order_ref[i]
        pair = lax.rem(prompt, pairs)
        null = prompt >= pairs
        counted = counts_ref[pair]
        size = jnp.where(null, 1, counted)
        target = base[pair] + jnp.where(null, counted, 0)

        def one(w, carry):
            for kv in range(2):
                pltpu.make_async_copy(
                    landed_ref.at[kv, pl.ds((first + w) * part, part)],
                    staged.at[kv, target + w],
                    in_sem.at[kv],
                ).start()
            return carry

        lax.fori_loop(0, size, one, 0)
        return first + size

    lax.fori_loop(0, prompts, fetch, jnp.int32(0))
    outs = []
    for kv, ref in enumerate((keys_ref, values_ref)):
        pltpu.make_async_copy(staged.at[kv], staged.at[kv], in_sem.at[kv]).wait()
        copy = pltpu.make_async_copy(staged.at[kv], ref.at[0], out_sem.at[kv])
        copy.start()
        outs.append(copy)
    for copy in outs:
        copy.wait()


def local(n, queries, keys, values, block_counts, last_tokens, pack_order, decode_slot):
    tokens, features = queries.shape
    here = tokens // BLOCK
    splits = n // HEADS
    part = BLOCK // splits
    blocks = here * n
    kind = queries.dtype
    smem = pl.BlockSpec(memory_space=pltpu.SMEM)
    vmem = pl.BlockSpec(memory_space=pltpu.VMEM)
    anywhere = pl.BlockSpec(memory_space=pl.ANY)
    dma = pltpu.SemaphoreType.DMA
    attended, landed = pl.pallas_call(
        functools.partial(exchange, n),
        out_shape=(
            jax.ShapeDtypeStruct((tokens, features), kind),
            jax.ShapeDtypeStruct((2, blocks * part, HEAD_DIM), kind),
        ),
        in_specs=[smem] * 3 + [vmem] * 3,
        out_specs=(vmem, anywhere),
        scratch_shapes=[
            pltpu.VMEM((BACK * BLOCK, features), kind),
            pltpu.VMEM((BACK * BLOCK, features), kind),
            pltpu.VMEM((2, BLOCK, features), kind),
            pltpu.VMEM((tokens, (BACK + here) * BLOCK), jnp.float32),
            dma((64,)),
            dma((2, BACK)),
            dma((2,)),
            dma((2,)),
            dma((2,)),
            dma((2, here)),
        ],
        compiler_params=pltpu.CompilerParams(
            collective_id=0, has_side_effects=True, vmem_limit_bytes=48 * 1024 * 1024
        ),
    )(block_counts, last_tokens, pack_order, queries, keys, values)
    cache = jax.ShapeDtypeStruct((1, blocks, part, HEAD_DIM), kind)
    cache_keys, cache_values = pl.pallas_call(
        reorder,
        out_shape=(cache, cache),
        in_specs=[smem] * 3 + [anywhere],
        out_specs=(anywhere, anywhere),
        scratch_shapes=[
            pltpu.VMEM((2, blocks, part, HEAD_DIM), kind),
            pltpu.SMEM(block_counts.shape, jnp.int32),
            pltpu.SMEM(block_counts.shape, jnp.int32),
            dma((2,)),
            dma((2,)),
        ],
    )(block_counts, pack_order, decode_slot, landed)
    return attended, cache_keys, cache_values


def solution(mesh):
    rows = P(("groups", "seq"), None)
    small = P("groups")
    cache = P(("groups", "seq"), None, None, None)
    return jax.shard_map(
        functools.partial(local, mesh.shape["seq"]),
        mesh=mesh,
        in_specs=(rows, rows, rows, small, small, small, small),
        out_specs=(rows, cache, cache),
        check_vma=False,
    )
```

time: 190 us -> 119 us (0.63)
  the two profiles are of different devices: /device:TPU:20 before, /device:TPU:25 now
where the time goes in v1:
time: 119 us
  Pallas kernels  112 us (94%)
  local copies, waits for them, and re-layouts  6.6 us (6%)
    pallas_call x1, Pallas kernels, local(): pl.pallas_call(functools.partial(exchange, n), out_shape=(jax.ShapeDtypeS...  108 us
    unnamed x13, local copies, waits for them, and re-layouts  6.6 us
    pallas_call x1, Pallas kernels, local(): pl.pallas_call(reorder, out_shape=(cache, cache), in_specs=[smem] * 3 + [...  3.74 us

profile of v1, /device:TPU:25, one launch (start us, length us, event | category | flops | bytes accessed | tf_op | source)
XLA Modules:
  0.0 119.0 jit_solution(8316598316115216779)
XLA Ops:
  0.6 0.0 copy-start
  0.6 1.2 %copy-done = bf16[256,2048]{1,0:T(8,128)(2,1)S(1)} copy-done((bf16[256,2048]{1,0:T(8,128)(2,1)S(1)}, bf16[256,2048]{1,0:T(8,128)(2,1)}, u32[]{:S(2)}) %copy-start) | copy-done | bytes 1048600
  1.9 0.0 copy-start.1
  1.9 1.2 %copy-done.1 = bf16[256,2048]{1,0:T(8,128)(2,1)S(1)} copy-done((bf16[256,2048]{1,0:T(8,128)(2,1)S(1)}, bf16[256,2048]{1,0:T(8,128)(2,1)}, u32[]{:S(2)}) %copy-start.1) | copy-done | bytes 1048600
  3.1 0.0 copy-start.2
  3.1 1.2 %copy-done.2 = bf16[256,2048]{1,0:T(8,128)(2,1)S(1)} copy-done((bf16[256,2048]{1,0:T(8,128)(2,1)S(1)}, bf16[256,2048]{1,0:T(8,128)(2,1)}, u32[]{:S(2)}) %copy-start.2) | copy-done | bytes 1048600
  4.3 0.0 copy-start.3
  4.3 0.7 copy-done.3
  5.0 0.0 copy-start.4
  5.0 0.7 copy-done.4
  5.6 0.0 copy-start.5
  5.6 0.7 copy-done.5
  6.3 108.0 %shard_map.94 = (bf16[256,2048]{1,0:T(8,128)(2,1)S(1)}, bf16[2,4096,128]{2,1,0:T(8,128)(2,1)}) custom-call(s32[8]{0:T(128)S(1)} %copy-done.3, s32[16]{0:T(128)S(1)} %copy-done.5, s32[16]{0:T(128)S(1)} %copy-done.4, bf16[256,2048]{1,0:T(8,128)(2,1)S(1)} %copy-done, bf16[256,2048]{1,0:T(8,128)(2,1)S(1)} %copy-done.1, bf16[256,2048]{1,0:T(8,128)(2,1)S(1)} %copy-done.2), custom_call_target="tpu_custom_call" | custom-call | tf_op jit(solution)/shard_map/pallas_call | solution.py:364
  114.3 3.7 %shard_map.95 = (bf16[1,32,128,128]{3,2,1,0:T(8,128)(2,1)}, bf16[1,32,128,128]{3,2,1,0:T(8,128)(2,1)}) custom-call(s32[8]{0:T(128)} %counts_ref.3, s32[16]{0:T(128)} %order_ref.3, s32[8]{0:T(128)} %slot_ref.1, bf16[2,4096,128]{2,1,0:T(8,128)(2,1)} %get-tuple-element.8.landed_ref), custom_call_target="tpu_custom_call" | custom-call | tf_op jit(solution)/shard_map/pallas_call | solution.py:389
  118.0 1.0 copy.11
Async XLA Ops:
  0.6 1.2 %copy-start = (bf16[256,2048]{1,0:T(8,128)(2,1)S(1)}, bf16[256,2048]{1,0:T(8,128)(2,1)}, u32[]{:S(2)}) copy-start(bf16[256,2048]{1,0:T(8,128)(2,1)} %q_ref.1) | copy-start | bytes 3145732
  1.9 1.2 %copy-start.1 = (bf16[256,2048]{1,0:T(8,128)(2,1)S(1)}, bf16[256,2048]{1,0:T(8,128)(2,1)}, u32[]{:S(2)}) copy-start(bf16[256,2048]{1,0:T(8,128)(2,1)} %k_ref.1) | copy-start | bytes 3145732
  3.1 1.2 %copy-start.2 = (bf16[256,2048]{1,0:T(8,128)(2,1)S(1)}, bf16[256,2048]{1,0:T(8,128)(2,1)}, u32[]{:S(2)}) copy-start(bf16[256,2048]{1,0:T(8,128)(2,1)} %v_ref.1) | copy-start | bytes 3145732
  4.3 0.7 copy-start.3
  5.0 0.7 copy-start.4
  5.6 0.7 copy-start.5

commit v2 on v1

v2 whole, which is shorter than its diff:
```python
import functools
import math

import jax
import jax.numpy as jnp
from jax import lax
from jax.experimental import pallas as pl
from jax.experimental.pallas import tpu as pltpu
from jax.sharding import PartitionSpec as P

HEADS = 16
HEAD_DIM = 128
BLOCK = 128
MAXB = 6
BACK = MAXB - 1
HIDDEN = -1e30
PLANE = 4
CHUNKS = 4
RELAY = BACK
ROUND = 2


def window_tables(counts_ref, tails_ref, order_ref, first, width):
    pairs = counts_ref.shape[0]
    prompts = order_ref.shape[0]

    def place(i, carry):
        start, docs, valids = carry
        prompt = order_ref[i]
        counted = counts_ref[lax.rem(prompt, pairs)]
        size = jnp.where(prompt < pairs, counted, 1)
        tail = tails_ref[prompt]
        end = start + size
        new_docs, new_valids = [], []
        for w in range(width):
            b = first + w
            inside = (start <= b) & (b < end)
            new_docs.append(jnp.where(inside, i, docs[w]))
            new_valids.append(
                jnp.where(inside, jnp.where(b + 1 == end, tail, BLOCK), valids[w])
            )
        return end, tuple(new_docs), tuple(new_valids)

    none = jnp.int32(-1)
    zero = jnp.int32(0)
    _, docs, valids = lax.fori_loop(
        0, prompts, place, (zero, (none,) * width, (zero,) * width)
    )
    return docs, valids


def exchange(
    n,
    counts_ref,
    tails_ref,
    order_ref,
    q_hbm,
    k_hbm,
    v_hbm,
    out_ref,
    landed_ref,
    q_ref,
    own,
    halo,
    relay,
    bias,
    halo_send,
    halo_recv,
    cache_sem,
    own_sem,
    load_sem,
):
    me = lax.axis_index("seq")
    role = lax.rem(me, PLANE)
    plane = me // PLANE
    planes = n // PLANE
    tokens, features = q_ref.shape
    here = tokens // BLOCK
    splits = n // HEADS
    part = BLOCK // splits
    wide = features // CHUNKS

    loads = [
        pltpu.make_async_copy(src, dst, load_sem.at[i])
        for i, (src, dst) in enumerate(
            ((k_hbm, own.at[0]), (v_hbm, own.at[1]), (q_hbm, q_ref))
        )
    ]
    for copy in loads:
        copy.start()

    barrier = pltpu.get_barrier_semaphore()

    def greet(r, carry):
        pl.semaphore_signal(
            barrier,
            inc=1,
            device_id={"seq": lax.rem(me + r, n)},
            device_id_type=pl.DeviceIdType.MESH,
        )
        return carry

    lax.fori_loop(1, n, greet, 0)
    loads[0].wait()
    loads[1].wait()
    pl.semaphore_wait(barrier, n - 1)

    pending = []

    def spot(block, c):
        return (
            slice(None),
            pl.ds(block * BLOCK, BLOCK),
            pl.ds(c * wide, wide),
        )

    def mine(block):
        return lambda c: own.at[spot(block, c)]

    def held(slot):
        if slot >= RELAY:
            return lambda c: relay.at[spot(slot - RELAY, c)]
        return lambda c: halo.at[spot(slot, c)]

    def start(cond, c, moves):
        copies = []
        for src, target, slot in moves:
            copy = pltpu.make_async_remote_copy(
                src_ref=src(c),
                dst_ref=held(slot)(c),
                send_sem=halo_send.at[len(pending)],
                recv_sem=halo_recv.at[slot, c],
                device_id={"seq": lax.rem(target + n, n)},
                device_id_type=pl.DeviceIdType.MESH,
            )
            pending.append((cond, copy))
            copies.append(copy)

        @pl.when(cond)
        def _():
            for copy in copies:
                copy.start()

    def await_slots(cond, c, slots):
        @pl.when(cond)
        def _():
            for slot in slots:
                ref = held(slot)(c)
                pltpu.make_async_copy(ref, ref, halo_recv.at[slot, c]).wait()

    more = plane < planes - 1
    late = plane > 0
    for c in range(CHUNKS):
        start((role == 3) & more, c, [(mine(0), me + 3, RELAY), (mine(1), me + 3, 0)])
        if c < ROUND:
            moves = [(mine(1), me - 2, RELAY + 1), (mine(0), me - 2, RELAY)]
        else:
            moves = [(mine(1), me + 2, 2), (mine(0), me + 2, 1)]
        start((role == 2) & more, c, moves)
        start((role == 1) & more, c, [(mine(1), me + 3, 0)])
        start(role == 1, c, [(mine(0), me + 1, 3), (mine(1), me + 1, 4)])
        start(role == 0, c, [(mine(1), me + 2, 2), (mine(0), me + 2, 1)])
        start(
            (role == 0) | (role == 2),
            c,
            [(mine(0), me + 1, 3), (mine(1), me + 1, 4)],
        )

    def piece(owner, block):
        head = owner // splits
        cols = pl.ds(pl.multiple_of(head * HEAD_DIM, HEAD_DIM), HEAD_DIM)
        if splits == 1:
            return own.at[:, :, cols]
        offset = pl.multiple_of(block * BLOCK + lax.rem(owner, splits) * part, part)
        return own.at[:, pl.ds(offset, part), cols]

    def place(block):
        if splits == 1:
            return landed_ref.at[:, pl.ds(pl.multiple_of(me * tokens, tokens), tokens)]
        return landed_ref.at[
            :, pl.ds(pl.multiple_of((me * here + block) * part, part), part)
        ]

    pieces = 1 if splits == 1 else here

    def give(s, carry):
        sign = 1 - 2 * lax.rem(s, 2)
        target = lax.rem(me + n // 2 + sign * ((s + 1) // 2), n)
        for block in range(pieces):
            pltpu.make_async_remote_copy(
                src_ref=piece(target, block),
                dst_ref=place(block),
                send_sem=cache_sem.at[0],
                recv_sem=cache_sem.at[1],
                device_id={"seq": target},
                device_id_type=pl.DeviceIdType.MESH,
            ).start()
        return carry

    cuts = [(n - 1) * i // CHUNKS for i in range(CHUNKS + 1)]

    docs, valids = window_tables(
        counts_ref, tails_ref, order_ref, me * here - BACK, BACK + here
    )
    row = lax.broadcasted_iota(jnp.int32, (BLOCK, BLOCK), 0)
    col = lax.broadcasted_iota(jnp.int32, (BLOCK, BLOCK), 1)
    for b in range(here):
        for w in range(BACK + here):
            if w > BACK + b:
                shade = jnp.full((BLOCK, BLOCK), HIDDEN, jnp.float32)
            else:
                limit = jnp.where(docs[w] == docs[BACK + b], valids[w], 0)
                seen = col < limit
                if w == BACK + b:
                    seen = seen & (col <= row)
                shade = jnp.where(seen, 0.0, HIDDEN)
            bias[b * BLOCK : (b + 1) * BLOCK, w * BLOCK : (w + 1) * BLOCK] = shade
    column = lax.broadcasted_iota(jnp.int32, (BLOCK, HEAD_DIM), 0)
    real = jnp.concatenate(
        [column < valids[BACK + b] for b in range(here)], axis=0
    )

    empty = jnp.zeros((BLOCK, features), halo.dtype)
    for slot, reach in ((0, 3), (1, 2), (2, 2), (3, 1), (4, 1)):

        @pl.when(me < reach)
        def _():
            for kv in range(2):
                halo[kv, slot * BLOCK : (slot + 1) * BLOCK, :] = empty

    loads[2].wait()

    factor = HEAD_DIM ** (-0.5) * math.log2(math.e)
    prior = BACK * BLOCK
    nt = (((1,), (1,)), ((), ()))

    def one_head(h, carry):
        cols = pl.ds(pl.multiple_of(h * HEAD_DIM, HEAD_DIM), HEAD_DIM)
        q = q_ref[:, cols]
        s1 = lax.dot_general(q, halo[0, :, cols], nt, preferred_element_type=jnp.float32)
        s2 = lax.dot_general(q, own[0, :, cols], nt, preferred_element_type=jnp.float32)
        s1 = s1 + bias[:, :prior]
        s2 = s2 + bias[:, prior:]
        peak = jnp.maximum(
            jnp.max(s1, axis=1, keepdims=True), jnp.max(s2, axis=1, keepdims=True)
        )
        w1 = jnp.exp2((s1 - peak) * factor)
        w2 = jnp.exp2((s2 - peak) * factor)
        total = jnp.sum(w1, axis=1, keepdims=True) + jnp.sum(w2, axis=1, keepdims=True)
        mixed = jnp.dot(
            w1.astype(jnp.bfloat16), halo[1, :, cols], preferred_element_type=jnp.float32
        ) + jnp.dot(
            w2.astype(jnp.bfloat16), own[1, :, cols], preferred_element_type=jnp.float32
        )
        out_ref[:, cols] = jnp.where(real, mixed / total, 0.0).astype(out_ref.dtype)
        return carry

    for c in range(CHUNKS):
        lax.fori_loop(cuts[c], cuts[c + 1], give, 0)
        if c < ROUND:
            await_slots((role == 0) & more, c, [RELAY, RELAY + 1])
            start(
                (role == 0) & more,
                c,
                [(held(RELAY + 1), me + PLANE, 2), (held(RELAY), me + PLANE, 1)],
            )
        await_slots((role == 2) & late, c, [RELAY, 0])
        start(
            (role == 2) & late, c, [(held(RELAY), me - 2 + n, 3), (held(0), me - 2 + n, 4)]
        )
        await_slots((role == 0) & late, c, [2, 3, 4])
        await_slots(role == 2, c, [2, 3, 4])
        start(
            (role == 2) | ((role == 0) & late),
            c,
            [(held(2), me + 1, 0), (held(3), me + 1, 1), (held(4), me + 1, 2)],
        )
        await_slots((role == 0) & late, c, [0, 1])
        await_slots(role == 1, c, [3, 4])
        await_slots((role == 1) & late, c, [0, 1, 2])
        await_slots(role == 2, c, [1])
        await_slots(role == 3, c, [0, 1, 2, 3, 4])
        each = HEADS // CHUNKS
        lax.fori_loop(c * each, (c + 1) * each, one_head, 0)

    copies = [
        pltpu.make_async_copy(piece(me, block), place(block), own_sem.at[block])
        for block in range(pieces)
    ]
    for copy in copies:
        copy.start()

    for cond, copy in pending:

        @pl.when(cond)
        def _():
            copy.wait_send()

    for copy in copies:
        copy.wait()
    others = landed_ref.shape[1] // n * (n - 1)
    ref = landed_ref.at[:, pl.ds(0, others)]
    pltpu.make_async_copy(ref, ref, cache_sem.at[0]).wait()
    pltpu.make_async_copy(ref, ref, cache_sem.at[1]).wait()


def reorder(
    counts_ref,
    order_ref,
    slot_ref,
    landed_ref,
    keys_ref,
    values_ref,
    staged,
    who,
    base,
    in_sem,
    out_sem,
):
    pairs = counts_ref.shape[0]
    prompts = order_ref.shape[0]
    blocks, part = staged.shape[1:3]

    def invert(p, carry):
        who[slot_ref[p]] = p
        return carry

    lax.fori_loop(0, pairs, invert, 0)

    def lay(s, first):
        p = who[s]
        base[p] = first
        return first + counts_ref[p] + 1

    lax.fori_loop(0, pairs, lay, jnp.int32(0))

    def fetch(i, first):
        prompt = order_ref[i]
        pair = lax.rem(prompt, pairs)
        null = prompt >= pairs
        counted = counts_ref[pair]
        size = jnp.where(null, 1, counted)
        target = base[pair] + jnp.where(null, counted, 0)

        def one(w, carry):
            for kv in range(2):
                pltpu.make_async_copy(
                    landed_ref.at[kv, pl.ds((first + w) * part, part)],
                    staged.at[kv, target + w],
                    in_sem.at[kv],
                ).start()
            return carry

        lax.fori_loop(0, size, one, 0)
        return first + size

    lax.fori_loop(0, prompts, fetch, jnp.int32(0))
    outs = []
    for kv, ref in enumerate((keys_ref, values_ref)):
        pltpu.make_async_copy(staged.at[kv], staged.at[kv], in_sem.at[kv]).wait()
        copy = pltpu.make_async_copy(staged.at[kv], ref.at[0], out_sem.at[kv])
        copy.start()
        outs.append(copy)
    for copy in outs:
        copy.wait()


def local(n, queries, keys, values, block_counts, last_tokens, pack_order, decode_slot):
    tokens, features = queries.shape
    here = tokens // BLOCK
    splits = n // HEADS
    part = BLOCK // splits
    blocks = here * n
    kind = queries.dtype
    smem = pl.BlockSpec(memory_space=pltpu.SMEM)
    vmem = pl.BlockSpec(memory_space=pltpu.VMEM)
    anywhere = pl.BlockSpec(memory_space=pl.ANY)
    dma = pltpu.SemaphoreType.DMA
    attended, landed = pl.pallas_call(
        functools.partial(exchange, n),
        out_shape=(
            jax.ShapeDtypeStruct((tokens, features), kind),
            jax.ShapeDtypeStruct((2, blocks * part, HEAD_DIM), kind),
        ),
        in_specs=[smem] * 3 + [anywhere] * 3,
        out_specs=(vmem, anywhere),
        scratch_shapes=[
            pltpu.VMEM((tokens, features), kind),
            pltpu.VMEM((2, tokens, features), kind),
            pltpu.VMEM((2, BACK * BLOCK, features), kind),
            pltpu.VMEM((2, 2 * BLOCK, features), kind),
            pltpu.VMEM((tokens, (BACK + here) * BLOCK), jnp.float32),
            dma((CHUNKS * 18,)),
            dma((BACK + 2, CHUNKS)),
            dma((2,)),
            dma((here,)),
            dma((3,)),
        ],
        compiler_params=pltpu.CompilerParams(
            collective_id=0, has_side_effects=True, vmem_limit_bytes=60 * 1024 * 1024
        ),
    )(block_counts, last_tokens, pack_order, queries, keys, values)
    cache = jax.ShapeDtypeStruct((1, blocks, part, HEAD_DIM), kind)
    cache_keys, cache_values = pl.pallas_call(
        reorder,
        out_shape=(cache, cache),
        in_specs=[smem] * 3 + [anywhere],
        out_specs=(anywhere, anywhere),
        scratch_shapes=[
            pltpu.VMEM((2, blocks, part, HEAD_DIM), kind),
            pltpu.SMEM(block_counts.shape, jnp.int32),
            pltpu.SMEM(block_counts.shape, jnp.int32),
            dma((2,)),
            dma((2,)),
        ],
    )(block_counts, pack_order, decode_slot, landed)
    return attended, cache_keys, cache_values


def solution(mesh):
    rows = P(("groups", "seq"), None)
    small = P("groups")
    cache = P(("groups", "seq"), None, None, None)
    return jax.shard_map(
        functools.partial(local, mesh.shape["seq"]),
        mesh=mesh,
        in_specs=(rows, rows, rows, small, small, small, small),
        out_specs=(rows, cache, cache),
        check_vma=False,
    )
```

time: 119 us -> 103 us (0.87)
  the two profiles are of different devices: /device:TPU:25 before, /device:TPU:18 now
where the time goes in v2:
time: 103 us
  Pallas kernels  101 us (98%)
    pallas_call x1, Pallas kernels, local(): pl.pallas_call(functools.partial(exchange, n), out_shape=(jax.ShapeDtypeS...  97.1 us
    pallas_call x1, Pallas kernels, local(): pl.pallas_call(reorder, out_shape=(cache, cache), in_specs=[smem] * 3 + [...  3.87 us

profile of v2, /device:TPU:18, one launch (start us, length us, event | category | flops | bytes accessed | tf_op | source)
XLA Modules:
  0.0 102.6 jit_solution(14094669101844625748)
XLA Ops:
  0.6 97.1 %shard_map.94 = (bf16[256,2048]{1,0:T(8,128)(2,1)}, bf16[2,4096,128]{2,1,0:T(8,128)(2,1)}) custom-call(s32[8]{0:T(128)} %counts_ref.3, s32[16]{0:T(128)} %tails_ref.1, s32[16]{0:T(128)} %order_ref.3, bf16[256,2048]{1,0:T(8,128)(2,1)} %q_hbm.1, bf16[256,2048]{1,0:T(8,128)(2,1)} %k_hbm.1, bf16[256,2048]{1,0:T(8,128)(2,1)} %v_hbm.1), custom_call_target="tpu_custom_call" | custom-call | tf_op jit(solution)/shard_map/pallas_call | solution.py:379
  97.8 0.0 copy-start
  97.8 3.9 %shard_map.95 = (bf16[1,32,128,128]{3,2,1,0:T(8,128)(2,1)}, bf16[1,32,128,128]{3,2,1,0:T(8,128)(2,1)}) custom-call(s32[8]{0:T(128)} %counts_ref.3, s32[16]{0:T(128)} %order_ref.3, s32[8]{0:T(128)} %slot_ref.1, bf16[2,4096,128]{2,1,0:T(8,128)(2,1)} %get-tuple-element.8.landed_ref), custom_call_target="tpu_custom_call" | custom-call | tf_op jit(solution)/shard_map/pallas_call | solution.py:404
  101.7 0.0 copy-done
  101.7 1.0 copy.11
Async XLA Ops:
  97.8 3.9 %copy-start = (bf16[256,2048]{1,0:T(8,128)(2,1)S(1)}, bf16[256,2048]{1,0:T(8,128)(2,1)}, u32[]{:S(2)}) copy-start(bf16[256,2048]{1,0:T(8,128)(2,1)} %get-tuple-element.14) | copy-start | bytes 3145732
